TPU v7x, 32 devices: a whole 2x2x4 slice. The times are simulated.
32 devices in a mesh: ia: 4 (over y, x), ja: 4 (over z), col: 2 (over core).
Axes of the slice: x: 2, y: 2, z: 4, core: 2. Of those that a mesh axis runs over, the one named last changes fastest.
Arguments:
- pair_rep: bfloat16 [512, 512, 128], P('ia', 'ja'), may hold values from -6 to 6
- norm_gain: float32 [128], replicated, may hold values from 0.1 to 1.9
- weights: bfloat16 [4, 128, 128], P(None, None, 'col'), may hold values from -0.5 to 0.5
- residue_mask: int32 [512], replicated, may hold values 0 or 1
- product_grad: bfloat16 [512, 128, 512], P('ia', 'col', 'ja'), may hold values from -1 to 1
Outputs:
- pair_grad: bfloat16 [512, 512, 128], P('ia', 'ja')
- weight_grads: float32 [4, 128, 128], P(None, None, 'col')
All inputs are finite; a program needn't handle non-finite values.
Results may differ from a plain program's by a relative error of at most 0.0067.
Values may be sent and summed in bfloat16 or wider, within the bound.
A program may use at most 128 MiB of HBM per device.

v0:
```python
import jax
import jax.numpy as jnp
from jax import lax
from jax.sharding import PartitionSpec as P

CLIP_LIMIT = 64.0


def gate_terms(incoming, linear, gate_pre, pair_valid):
    sigmoid_gate = jax.nn.sigmoid(gate_pre)
    through = incoming * pair_valid
    return (through * sigmoid_gate, through * linear * sigmoid_gate * (1.0 - sigmoid_gate))


def on_device(pair_rep, norm_gain, weights, residue_mask, product_grad):
    row_count = pair_rep.shape[0]
    col_count = pair_rep.shape[1]
    row_first = lax.axis_index("ia") * row_count
    col_first = lax.axis_index("ja") * col_count
    validity = residue_mask.astype(jnp.float32)
    row_valid = lax.dynamic_slice_in_dim(validity, row_first, row_count)
    col_valid = lax.dynamic_slice_in_dim(validity, col_first, col_count)
    pair_valid = row_valid[:, None, None] * col_valid[None, None, :]
    floats = pair_rep.astype(jnp.float32)
    centred = floats - jnp.mean(floats, axis=-1, keepdims=True)
    inv_std = lax.rsqrt(jnp.mean(centred * centred, axis=-1, keepdims=True) + 1e-05)
    unit_rows = centred * inv_std
    normed = (unit_rows * norm_gain).astype(jnp.bfloat16)
    projected = jnp.einsum("ikd,wdc->wick", normed, weights, preferred_element_type=jnp.float32)
    left_side = (pair_valid * jax.nn.sigmoid(projected[1]) * projected[0]).astype(jnp.bfloat16)
    right_side = (pair_valid * jax.nn.sigmoid(projected[3]) * projected[2]).astype(jnp.bfloat16)
    row_panel = lax.all_gather(product_grad, "ja", axis=2, tiled=True)
    panel_part = row_panel
    grad_left = jnp.einsum(
        "icj,jck->ick",
        panel_part,
        lax.all_gather(right_side, "ia", axis=0, tiled=True),
        preferred_element_type=jnp.float32,
    )
    panel_part = row_panel
    grad_right = lax.psum_scatter(
        jnp.einsum("icj,ick->jck", panel_part, left_side, preferred_element_type=jnp.float32),
        "ia",
        scatter_dimension=0,
        tiled=True,
    )
    lin_a, gate_a = gate_terms(grad_left, projected[0], projected[1], pair_valid)
    lin_b, gate_b = gate_terms(grad_right, projected[2], projected[3], pair_valid)
    proj_grads = jnp.stack([lin_a, gate_a, lin_b, gate_b]).astype(jnp.bfloat16)
    grad_part = jnp.einsum("ikd,wick->wdc", normed, proj_grads, preferred_element_type=jnp.float32)
    input_part = jnp.einsum(
        "wick,wdc->ikd", proj_grads, weights, preferred_element_type=jnp.float32
    )
    normed_grad = lax.psum(input_part, "col")
    scaled = normed_grad * norm_gain
    pair_grad = inv_std * (
        scaled
        - jnp.mean(scaled, axis=-1, keepdims=True)
        - unit_rows * jnp.mean(scaled * unit_rows, axis=-1, keepdims=True)
    )
    summed = lax.psum(grad_part, ("ia", "ja"))
    squares = lax.psum(jnp.sum(summed * summed), "col")
    factor = jnp.minimum(1.0, CLIP_LIMIT * lax.rsqrt(squares + 1e-06))
    weight_grads = summed * factor
    return (pair_grad.astype(jnp.bfloat16), weight_grads)


def solution(mesh):
    placed = (P("ia", "ja", None), P(), P(None, None, "col"), P(), P("ia", "col", "ja"))
    return jax.shard_map(
        on_device,
        mesh=mesh,
        in_specs=placed,
        out_specs=(P("ia", "ja", None), P(None, None, "col")),
        check_vma=False,
    )
```

profile of v0, /device:TPU:0, one launch (start us, length us, event | category | flops | bytes accessed | tf_op | source)
XLA Modules:
  0.0 660.3 jit_solution(14896707460684824877)
XLA Ops:
  7.2 4.3 copy.18
  11.8 3.5 convert_reduce_fusion
  15.3 4.8 fusion.10
  20.2 4.7 convolution_bitcast_fusion
  24.9 5.9 copy-done.1
  30.8 2.6 multiply_convert_fusion.5
  33.9 129.6 %all-gather.5.cloned.1.call-done = bf16[128,64,512]{2,0,1:T(8,128)(2,1)} async-done(((bf16[128,64,128]{2,0,1:T(8,128)(2,1)}), bf16[128,64,512]{2,0,1:T(8,128)(2,1)}) %all-gather.5.cloned.1.call-update) | async-done | bytes 8388624 | tf_op jit(solution)/shard_map/all_gather | solution.py:32
  163.5 87.5 %all-gather.3.cloned.1.call-done = bf16[512,64,128]{2,1,0:T(8,128)(2,1)} async-done(((bf16[128,64,128]{2,1,0:T(8,128)(2,1)}), bf16[512,64,128]{2,1,0:T(8,128)(2,1)}) %all-gather.3.cloned.1.call-update) | async-done | bytes 8388624 | tf_op jit(solution)/shard_map/all_gather | solution.py:37
  251.0 25.2 %fusion.11 = f32[64,128,128]{2,1,0:T(8,128)} fusion(bf16[128,64,512]{2,0,1:T(8,128)(2,1)} %all-gather.5.cloned.1.call-done, bf16[512,64,128]{2,1,0:T(8,128)(2,1)} %all-gather.3.cloned.1.call-done), kind=kOutput, calls=%fused_computation.15 | convolution fusion | flops 1073741824 | bytes 20971520 | tf_op jit(solution)/shard_map/icj,jck->ick/dot_general | solution.py:34
  276.2 5.4 copy.20
  281.6 6.8 %fusion.28 = (bf16[1,128,64,128]{3,2,1,0:T(8,128)(2,1)S(1)}, bf16[1,128,64,128]{3,2,1,0:T(8,128)(2,1)}, bf16[128,64,128]{2,1,0:T(8,128)(2,1)S(1)}) fusion(f32[64,128,128]{1,0,2:T(8,128)} %copy.20, f32[128,128]{1,0:T(8,128)S(1)} %broadcast_multiply_fusion.1, f32[4,128,64,128]{3,2,0,1:T(8,128)} %copy-done.1), kind=kLoop, calls=%fused_computation.43 | loop fusion | flops 14680064 | bytes 18939904 | tf_op jit(solution)/shard_map/stack | solution.py:49
  288.5 14.1 %fusion.32 = f32[64,128,512]{2,1,0:T(8,128)} fusion(bf16[128,64,512]{2,0,1:T(8,128)(2,1)} %all-gather.5.cloned.1.call-done, bf16[128,64,128]{2,1,0:T(8,128)(2,1)S(1)} %get-tuple-element.8), kind=kOutput, calls=%fused_computation.47 | convolution fusion | flops 1073741824 | bytes 27262976 | tf_op jit(solution)/shard_map/icj,ick->jck/dot_general | solution.py:42
  302.6 16.6 %copy.23 = f32[64,128,512]{1,0,2:T(8,128)} copy(f32[64,128,512]{2,1,0:T(8,128)} %fusion.32) | data formatting | bytes 33554432 | tf_op jit(solution)/shard_map/icj,ick->jck/dot_general | solution.py:42
  319.2 153.8 %reduce-scatter.2.cloned.1.call-done = f32[128,64,128]{2,1,0:T(8,128)} async-done(((f32[512,64,128]{2,1,0:T(8,128)}), f32[128,64,128]{2,1,0:T(8,128)}) %reduce-scatter.2.cloned.1.call-update) | async-done | bytes 4194320 | tf_op jit(solution)/shard_map/reduce_scatter | solution.py:41
  473.1 6.0 fusion.30
  481.1 5.4 fusion.34
  486.6 6.5 convolution_bitcast_fusion.1
  493.1 99.0 %all-reduce.5.cloned.1.call-done = f32[4,128,64]{1,2,0:T(8,128)} async-done(((f32[4,128,64]{1,2,0:T(8,128)}), f32[4,128,64]{1,2,0:T(8,128)}) %all-reduce.5.cloned.1.call-update) | async-done | bytes 131088 | tf_op jit(solution)/shard_map/psum | solution.py:61
  592.1 1.5 multiply_reduce_fusion.1
  593.7 3.1 psum.23
  597.4 1.6 broadcast_multiply_fusion
  599.0 32.2 %all-reduce.3.cloned.1.call-done = f32[128,128,128]{2,1,0:T(8,128)} async-done(((f32[128,128,128]{2,1,0:T(8,128)}), f32[128,128,128]{2,1,0:T(8,128)}) %all-reduce.3.cloned.1.call-update) | async-done | bytes 8388624 | tf_op jit(solution)/shard_map/psum | solution.py:54
  631.2 11.6 %multiply_reduce_fusion = (f32[128,128]{1,0:T(8,128)S(1)}, f32[128,128]{1,0:T(8,128)S(1)}) fusion(f32[128,128,128]{2,1,0:T(8,128)} %all-reduce.3.cloned.1.call-done, f32[128]{0:T(128)S(1)} %copy-done.9, f32[128,128]{1,0:T(8,128)S(1)} %add_rsqrt_fusion, f32[128,128]{1,0:T(8,128)S(1)} %broadcast_multiply_fusion.4, bf16[128,128,128]{2,1,0:T(8,128)(2,1)} %param.5), kind=kLoop, calls=%fused_computation.17 | loop fusion | flops 14647296 | bytes 12845568 | tf_op jit(solution)/shard_map/reduce_sum | solution.py:58
  642.8 10.7 %fusion.9 = bf16[128,128,128]{2,1,0:T(8,128)(2,1)} fusion(bf16[128,128,128]{2,1,0:T(8,128)(2,1)S(1)} %copy-done.4, f32[128,128,128]{2,1,0:T(8,128)S(1)} %copy-done.5, f32[128,128]{1,0:T(8,128)S(1)} %get-tuple-element.11, f32[128,128]{1,0:T(8,128)S(1)} %get-tuple-element.12, f32[128]{0:T(128)S(1)} %copy-done.9, f32[128,128]{1,0:T(8,128)S(1)} %add_rsqrt_fusion, ...), kind=kLoop, calls=%fused_computation.12 | loop fusion | flops 18874368 | bytes 17039872 | tf_op jit(solution)/shard_map/convert_element_type | solution.py:65
  (37 shorter events, 3.0 us)
Async XLA Ops:
  7.2 13.0 %copy-start = (bf16[4,128,64]{1,2,0:T(8,128)(2,1)S(1)}, bf16[4,128,64]{1,2,0:T(8,128)(2,1)}, u32[]{:S(2)}) copy-start(bf16[4,128,64]{1,2,0:T(8,128)(2,1)} %param.7) | copy-start | bytes 196612
  7.2 4.4 copy-start.10
  7.2 156.3 %all-gather.5.cloned.1.call-start = ((), (), s32[]{:S(2)}) async-start(), calls=%async_computation.2 | async-start | bytes 10485760 | tf_op jit(solution)/shard_map/all_gather | solution.py:32
  11.5 239.5 %all-gather.3.cloned.1.call-start = ((), (), s32[]{:S(2)}) async-start(), calls=%async_computation.1 | async-start | bytes 10485760 | tf_op jit(solution)/shard_map/all_gather | solution.py:37
  11.6 3.7 copy-start.2
  11.8 8.4 %copy-start.9 = (f32[128]{0:T(128)S(1)}, f32[128]{0:T(128)}, u32[]{:S(2)}) copy-start(f32[128]{0:T(128)} %param.6) | copy-start | bytes 1540
  24.9 5.9 copy-start.1
  33.4 439.6 %reduce-scatter.2.cloned.1.call-start = ((), (), s32[]{:S(2)}) async-start(), calls=%async_computation.3 | async-start | bytes 20971520 | tf_op jit(solution)/shard_map/reduce_scatter | solution.py:41
  319.2 272.9 %all-reduce.5.cloned.1.call-start = ((), (), s32[]{:S(2)}) async-start(), calls=%async_computation.5 | async-start | bytes 262144 | tf_op jit(solution)/shard_map/psum | solution.py:61
  473.1 8.0 %copy-start.3 = (bf16[128,128,128]{2,1,0:T(8,128)(2,1)S(1)}, bf16[128,128,128]{2,1,0:T(8,128)(2,1)}, u32[]{:S(2)}) copy-start(bf16[128,128,128]{2,1,0:T(8,128)(2,1)} %param.5) | copy-start | bytes 12582916
  473.1 8.0 %copy-start.6 = (bf16[1,128,64,128]{3,2,1,0:T(8,128)(2,1)S(1)}, bf16[1,128,64,128]{3,2,1,0:T(8,128)(2,1)}, u32[]{:S(2)}) copy-start(bf16[1,128,64,128]{3,2,1,0:T(8,128)(2,1)} %get-tuple-element.5) | copy-start | bytes 6291460
  479.1 1.3 copy-start.7
  479.1 2.0 copy-start.8
  486.6 144.6 %all-reduce.3.cloned.1.call-start = ((), (), s32[]{:S(2)}) async-start(), calls=%async_computation.4 | async-start | bytes 16777216 | tf_op jit(solution)/shard_map/psum | solution.py:54
  631.2 11.6 %copy-start.4 = (bf16[128,128,128]{2,1,0:T(8,128)(2,1)S(1)}, bf16[128,128,128]{2,1,0:T(8,128)(2,1)}, u32[]{:S(2)}) copy-start(bf16[128,128,128]{2,1,0:T(8,128)(2,1)} %param.5) | copy-start | bytes 12582916
  631.2 11.6 %copy-start.5 = (f32[128,128,128]{2,1,0:T(8,128)S(1)}, f32[128,128,128]{2,1,0:T(8,128)}, u32[]{:S(2)}) copy-start(f32[128,128,128]{2,1,0:T(8,128)} %all-reduce.3.cloned.1.call-done) | copy-start | bytes 25165828
Sparse Core Ops, SparseCore 0:
  11.6 151.8 all-gather.4
  165.4 85.6 all-gather.2
  319.3 153.7 reduce-scatter.1
  486.7 105.3 all-reduce.4
  594.4 36.6 all-reduce.2
where the time goes:
time: 668 us; the launch traced here: 660 us
  waiting for transfers between devices  502 us (75%)
  matrix products  55.9 us (8%)
  other arithmetic  49.3 us (7%)
  local copies, waits for them, and re-layouts  34.2 us (5%)
  between operations  14.9 us (2%)
    reduce_scatter x1, waiting for transfers between devices, on_device(): lax.psum_scatter(jnp.einsum('icj,ick->jck', panel_part, left_side, prefer...  154 us
    all_gather x1, waiting for transfers between devices, on_device(): row_panel = lax.all_gather(product_grad, 'ja', axis=2, tiled=True)  130 us
    psum x1, waiting for transfers between devices, on_device(): summed = lax.psum(grad_part, ('ia', 'ja'))  99 us
    all_gather x1, waiting for transfers between devices, on_device(): lax.all_gather(right_side, 'ia', axis=0, tiled=True)  87.5 us
    psum x1, waiting for transfers between devices, on_device(): normed_grad = lax.psum(input_part, 'col')  32.2 us
    dot_general x1, matrix products, on_device(): jnp.einsum('icj,jck->ick', panel_part, lax.all_gather(right_side, 'ia', a...  25.2 us
    dot_general x1, local copies, waits for them, and re-layouts, on_device(): jnp.einsum('icj,ick->jck', panel_part, left_side, preferred_element_type=...  16.6 us
    dot_general x1, matrix products, on_device(): jnp.einsum('icj,ick->jck', panel_part, left_side, preferred_element_type=...  14.1 us
  transfers between devices with their start and end apart: 5, of which 5 were waited for; matrix products, arithmetic and copies ran while one was open for 4% of the time, Pallas kernels for 0%

commit v1 on v0

--- a/solution.py
+++ b/solution.py
@@ -4,6 +4,10 @@
 from jax.sharding import PartitionSpec as P
 
 CLIP_LIMIT = 64.0
+
+
+def change_set(x_part):
+    return jnp.sum(jax.lax.all_gather(x_part, ("ia", "ja")), axis=0)
 
 
 def gate_terms(incoming, linear, gate_pre, pair_valid):
@@ -58,7 +62,7 @@
         - jnp.mean(scaled, axis=-1, keepdims=True)
         - unit_rows * jnp.mean(scaled * unit_rows, axis=-1, keepdims=True)
     )
-    summed = lax.psum(grad_part, ("ia", "ja"))
+    summed = change_set(grad_part)
     squares = lax.psum(jnp.sum(summed * summed), "col")
     factor = jnp.minimum(1.0, CLIP_LIMIT * lax.rsqrt(squares + 1e-06))
     weight_grads = summed * factor

time: 668 us -> 623 us (0.933)
  waiting for transfers between devices: 502 us -> 457 us
    psum x1 -> x0, waiting for transfers between devices: 99 us -> none  [on_device(): summed = lax.psum(grad_part, ('ia', 'ja'))]
    all_gather x0 -> x1, waiting for transfers between devices: none -> 54.1 us  [change_set(): return jnp.sum(jax.lax.all_gather(x_part, ('ia', 'ja')), axis=0)]
where the time goes in v1:
time: 623 us; the launch traced here: 615 us
  waiting for transfers between devices  457 us (73%)
  matrix products  55.9 us (9%)
  other arithmetic  49.3 us (8%)
  local copies, waits for them, and re-layouts  34.2 us (5%)
  between operations  14.9 us (2%)
    reduce_scatter x1, waiting for transfers between devices, on_device(): lax.psum_scatter(jnp.einsum('icj,ick->jck', panel_part, left_side, prefer...  154 us
    all_gather x1, waiting for transfers between devices, on_device(): row_panel = lax.all_gather(product_grad, 'ja', axis=2, tiled=True)  130 us
    all_gather x1, waiting for transfers between devices, on_device(): lax.all_gather(right_side, 'ia', axis=0, tiled=True)  87.5 us
    all_gather x1, waiting for transfers between devices, change_set(): return jnp.sum(jax.lax.all_gather(x_part, ('ia', 'ja')), axis=0)  54.1 us
    psum x1, waiting for transfers between devices, on_device(): normed_grad = lax.psum(input_part, 'col')  32 us
    dot_general x1, matrix products, on_device(): jnp.einsum('icj,jck->ick', panel_part, lax.all_gather(right_side, 'ia', a...  25.2 us
    dot_general x1, local copies, waits for them, and re-layouts, on_device(): jnp.einsum('icj,ick->jck', panel_part, left_side, preferred_element_type=...  16.6 us
    dot_general x1, matrix products, on_device(): jnp.einsum('icj,ick->jck', panel_part, left_side, preferred_element_type=...  14.1 us
  transfers between devices with their start and end apart: 5, of which 5 were waited for; matrix products, arithmetic and copies ran while one was open for 4% of the time, Pallas kernels for 0%

profile of v1, /device:TPU:0, one launch (start us, length us, event | category | flops | bytes accessed | tf_op | source)
XLA Modules:
  0.0 615.1 jit_solution(763372565973488246)
XLA Ops:
  7.2 4.3 copy.18
  11.8 3.5 convert_reduce_fusion
  15.3 4.8 fusion.10
  20.2 4.7 convolution_bitcast_fusion
  24.9 5.9 copy-done.1
  30.8 2.6 multiply_convert_fusion.5
  33.9 129.6 %all-gather.7.cloned.1.call-done = bf16[128,64,512]{2,0,1:T(8,128)(2,1)} async-done(((bf16[128,64,128]{2,0,1:T(8,128)(2,1)}), bf16[128,64,512]{2,0,1:T(8,128)(2,1)}) %all-gather.7.cloned.1.call-update) | async-done | bytes 8388624 | tf_op jit(solution)/shard_map/all_gather | solution.py:36
  163.5 87.5 %all-gather.5.cloned.1.call-done = bf16[512,64,128]{2,1,0:T(8,128)(2,1)} async-done(((bf16[128,64,128]{2,1,0:T(8,128)(2,1)}), bf16[512,64,128]{2,1,0:T(8,128)(2,1)}) %all-gather.5.cloned.1.call-update) | async-done | bytes 8388624 | tf_op jit(solution)/shard_map/all_gather | solution.py:41
  251.0 25.2 %fusion.11 = f32[64,128,128]{2,1,0:T(8,128)} fusion(bf16[128,64,512]{2,0,1:T(8,128)(2,1)} %all-gather.7.cloned.1.call-done, bf16[512,64,128]{2,1,0:T(8,128)(2,1)} %all-gather.5.cloned.1.call-done), kind=kOutput, calls=%fused_computation.15 | convolution fusion | flops 1073741824 | bytes 20971520 | tf_op jit(solution)/shard_map/icj,jck->ick/dot_general | solution.py:38
  276.2 5.4 copy.20
  281.6 6.8 %fusion.28 = (bf16[1,128,64,128]{3,2,1,0:T(8,128)(2,1)S(1)}, bf16[1,128,64,128]{3,2,1,0:T(8,128)(2,1)}, bf16[128,64,128]{2,1,0:T(8,128)(2,1)S(1)}) fusion(f32[64,128,128]{1,0,2:T(8,128)} %copy.20, f32[128,128]{1,0:T(8,128)S(1)} %broadcast_multiply_fusion.1, f32[4,128,64,128]{3,2,0,1:T(8,128)} %copy-done.1), kind=kLoop, calls=%fused_computation.43 | loop fusion | flops 14680064 | bytes 18939904 | tf_op jit(solution)/shard_map/stack | solution.py:53
  288.5 14.1 %fusion.32 = f32[64,128,512]{2,1,0:T(8,128)} fusion(bf16[128,64,512]{2,0,1:T(8,128)(2,1)} %all-gather.7.cloned.1.call-done, bf16[128,64,128]{2,1,0:T(8,128)(2,1)S(1)} %get-tuple-element.8), kind=kOutput, calls=%fused_computation.47 | convolution fusion | flops 1073741824 | bytes 27262976 | tf_op jit(solution)/shard_map/icj,ick->jck/dot_general | solution.py:46
  302.6 16.6 %copy.23 = f32[64,128,512]{1,0,2:T(8,128)} copy(f32[64,128,512]{2,1,0:T(8,128)} %fusion.32) | data formatting | bytes 33554432 | tf_op jit(solution)/shard_map/icj,ick->jck/dot_general | solution.py:46
  319.2 153.8 %reduce-scatter.2.cloned.1.call-done = f32[128,64,128]{2,1,0:T(8,128)} async-done(((f32[512,64,128]{2,1,0:T(8,128)}), f32[128,64,128]{2,1,0:T(8,128)}) %reduce-scatter.2.cloned.1.call-update) | async-done | bytes 4194320 | tf_op jit(solution)/shard_map/reduce_scatter | solution.py:45
  473.1 6.0 fusion.30
  479.2 1.3 copy-done.7
  481.1 5.4 fusion.34
  486.6 6.5 %convolution_bitcast_fusion.1 = f32[128,128,128]{2,1,0:T(8,128)} fusion(bf16[1,128,64,128]{3,2,1,0:T(8,128)(2,1)} %copy-done.8, bf16[1,128,64,128]{3,2,1,0:T(8,128)(2,1)} %copy-done.7, bf16[1,128,64,128]{3,2,1,0:T(8,128)(2,1)} %get-tuple-element.5, bf16[1,128,64,128]{3,2,1,0:T(8,128)(2,1)S(1)} %get-tuple-element.4, bf16[4,128,64]{1,2,0:T(8,128)(2,1)S(1)} %copy-done), kind=kOutput, calls=%fused_computation.42 | convolution fusion | flops 1086324736 | bytes 16842752 | tf_op jit(solution)/shard_map/wick,wdc->ikd/dot_general | solution.py:55
  493.1 54.1 %all-gather.9.cloned.1.call-done = f32[64,128,64]{1,2,0:T(8,128)} async-done(((f32[4,128,64]{1,2,0:T(8,128)}), f32[64,128,64]{1,2,0:T(8,128)}) %all-gather.9.cloned.1.call-update) | async-done | bytes 2097168 | tf_op jit(solution)/shard_map/all_gather | solution.py:10
  547.2 1.7 reduce_sum.58
  549.5 3.1 psum.15
  554.0 32.0 %all-reduce.2.cloned.1.call-done = f32[128,128,128]{2,1,0:T(8,128)} async-done(((f32[128,128,128]{2,1,0:T(8,128)}), f32[128,128,128]{2,1,0:T(8,128)}) %all-reduce.2.cloned.1.call-update) | async-done | bytes 8388624 | tf_op jit(solution)/shard_map/psum | solution.py:58
  586.0 11.6 %multiply_reduce_fusion = (f32[128,128]{1,0:T(8,128)S(1)}, f32[128,128]{1,0:T(8,128)S(1)}) fusion(f32[128,128,128]{2,1,0:T(8,128)} %all-reduce.2.cloned.1.call-done, f32[128]{0:T(128)S(1)} %copy-done.9, f32[128,128]{1,0:T(8,128)S(1)} %add_rsqrt_fusion, f32[128,128]{1,0:T(8,128)S(1)} %broadcast_multiply_fusion.4, bf16[128,128,128]{2,1,0:T(8,128)(2,1)} %param.5), kind=kLoop, calls=%fused_computation.17 | loop fusion | flops 14647296 | bytes 12845568 | tf_op jit(solution)/shard_map/reduce_sum | solution.py:62
  597.6 10.7 %fusion.9 = bf16[128,128,128]{2,1,0:T(8,128)(2,1)} fusion(bf16[128,128,128]{2,1,0:T(8,128)(2,1)S(1)} %copy-done.4, f32[128,128,128]{2,1,0:T(8,128)S(1)} %copy-done.5, f32[128,128]{1,0:T(8,128)S(1)} %get-tuple-element.11, f32[128,128]{1,0:T(8,128)S(1)} %get-tuple-element.12, f32[128]{0:T(128)S(1)} %copy-done.9, f32[128,128]{1,0:T(8,128)S(1)} %add_rsqrt_fusion, ...), kind=kLoop, calls=%fused_computation.12 | loop fusion | flops 18874368 | bytes 17039872 | tf_op jit(solution)/shard_map/convert_element_type | solution.py:69
  (38 shorter events, 3.0 us)
Async XLA Ops:
  7.2 13.0 %copy-start = (bf16[4,128,64]{1,2,0:T(8,128)(2,1)S(1)}, bf16[4,128,64]{1,2,0:T(8,128)(2,1)}, u32[]{:S(2)}) copy-start(bf16[4,128,64]{1,2,0:T(8,128)(2,1)} %param.7) | copy-start | bytes 196612
  7.2 4.4 copy-start.10
  7.2 156.3 %all-gather.7.cloned.1.call-start = ((), (), s32[]{:S(2)}) async-start(), calls=%async_computation.2 | async-start | bytes 10485760 | tf_op jit(solution)/shard_map/all_gather | solution.py:36
  11.5 239.5 %all-gather.5.cloned.1.call-start = ((), (), s32[]{:S(2)}) async-start(), calls=%async_computation.1 | async-start | bytes 10485760 | tf_op jit(solution)/shard_map/all_gather | solution.py:41
  11.6 3.7 copy-start.2
  11.8 8.4 %copy-start.9 = (f32[128]{0:T(128)S(1)}, f32[128]{0:T(128)}, u32[]{:S(2)}) copy-start(f32[128]{0:T(128)} %param.6) | copy-start | bytes 1540
  24.9 5.9 copy-start.1
  33.4 439.6 %reduce-scatter.2.cloned.1.call-start = ((), (), s32[]{:S(2)}) async-start(), calls=%async_computation.3 | async-start | bytes 20971520 | tf_op jit(solution)/shard_map/reduce_scatter | solution.py:45
  319.2 228.0 %all-gather.9.cloned.1.call-start = ((), (), s32[]{:S(2)}) async-start(), calls=%async_computation.5 | async-start | bytes 2228224 | tf_op jit(solution)/shard_map/all_gather | solution.py:10
  473.1 8.0 %copy-start.3 = (bf16[128,128,128]{2,1,0:T(8,128)(2,1)S(1)}, bf16[128,128,128]{2,1,0:T(8,128)(2,1)}, u32[]{:S(2)}) copy-start(bf16[128,128,128]{2,1,0:T(8,128)(2,1)} %param.5) | copy-start | bytes 12582916
  473.1 8.0 %copy-start.6 = (bf16[1,128,64,128]{3,2,1,0:T(8,128)(2,1)S(1)}, bf16[1,128,64,128]{3,2,1,0:T(8,128)(2,1)}, u32[]{:S(2)}) copy-start(bf16[1,128,64,128]{3,2,1,0:T(8,128)(2,1)} %get-tuple-element.5) | copy-start | bytes 6291460
  479.1 1.3 copy-start.7
  479.1 2.0 copy-start.8
  486.6 99.4 %all-reduce.2.cloned.1.call-start = ((), (), s32[]{:S(2)}) async-start(), calls=%async_computation.4 | async-start | bytes 16777216 | tf_op jit(solution)/shard_map/psum | solution.py:58
  586.0 11.6 %copy-start.4 = (bf16[128,128,128]{2,1,0:T(8,128)(2,1)S(1)}, bf16[128,128,128]{2,1,0:T(8,128)(2,1)}, u32[]{:S(2)}) copy-start(bf16[128,128,128]{2,1,0:T(8,128)(2,1)} %param.5) | copy-start | bytes 12582916
  586.0 11.6 %copy-start.5 = (f32[128,128,128]{2,1,0:T(8,128)S(1)}, f32[128,128,128]{2,1,0:T(8,128)}, u32[]{:S(2)}) copy-start(f32[128,128,128]{2,1,0:T(8,128)} %all-reduce.2.cloned.1.call-done) | copy-start | bytes 25165828
Sparse Core Ops, SparseCore 0:
  11.6 151.8 all-gather.6
  165.4 85.6 all-gather.4
  319.3 153.7 reduce-scatter.1
  486.7 60.4 all-gather.8
  549.5 36.4 all-reduce.1
